TPU v7x, 32 devices: a whole 2x2x4 slice. The times are simulated.
32 devices in a mesh: row: 4 (over y, x), col: 8 (over z, core).
Axes of the slice: x: 2, y: 2, z: 4, core: 2. Of those that a mesh axis runs over, the one named last changes fastest.
Arguments:
- old_residual: float32 [1024, 16384], P(('row', 'col')), may hold values from -6 to 6
- group_map: int32 [32, 4], replicated, may hold values from 0 to 127, as said below
- q_factor: float32 [16384, 32], P('col', 'row'), may hold values from -0.046875 to 0.046875
Outputs:
- relaid: float32 [1024, 16384], P('row', 'col')
- projection: float32 [32, 1024], P(None, ('row', 'col'))
- row_norms: float32 [1024], P(('row', 'col'))
Inputs may be any that keep to these rules, and one draw needn't show every extreme that they name: `group_map`: all entries together are each group id 0 to 127 once; row d (old device d) holds exactly one id of each range k * 32 to (k + 1) * 32 - 1, in any slot order.
All inputs are finite; a program needn't handle non-finite values.
Results may differ from a plain program's by a relative error of at most 0.00007.
Values sent between devices are 32-bit elements; how exact they have to be, the bound alone decides.
A program may use at most 64 MiB of HBM per device.

v0:
```python
import jax
import jax.numpy as jnp
from jax import lax
from jax.sharding import PartitionSpec as P

epsilon = 1e-06


def on_device(old_residual, group_map, q_factor):
    row_count = lax.axis_size("row")
    column_count = lax.axis_size("col")
    devices_all = row_count * column_count
    my_row = lax.axis_index("row")
    my_column = lax.axis_index("col")
    position = my_row * column_count + my_column
    group_rows = old_residual.shape[0] // row_count
    full_width = old_residual.shape[1]
    block_width = full_width // column_count
    own_ids = lax.dynamic_index_in_dim(group_map, position, 0, keepdims=False)
    sending = jnp.argsort(own_ids)
    stored = jnp.take(old_residual.reshape(row_count, group_rows, full_width), sending, axis=0)
    pieces = stored.reshape(row_count, group_rows, column_count, block_width).transpose(0, 2, 1, 3)
    flat_pieces = pieces.reshape(devices_all, group_rows, block_width)
    received = lax.all_to_all(flat_pieces, ("row", "col"), split_axis=0, concat_axis=0, tiled=True)
    sorted_map = jnp.sort(group_map, axis=1)
    arriving_ids = lax.dynamic_index_in_dim(sorted_map, my_row, 1, keepdims=False)
    placement = jnp.argsort(arriving_ids)
    arranged = jnp.take(received, placement, axis=0)
    relaid_block = arranged.reshape(devices_all * group_rows, block_width)
    factor_full = lax.all_gather(q_factor, "row", axis=1, tiled=True)
    projected_share = lax.psum_scatter(
        jnp.dot(
            relaid_block,
            factor_full,
            precision=lax.Precision.HIGHEST,
            preferred_element_type=jnp.float32,
        ),
        "col",
        scatter_dimension=0,
        tiled=True,
    )
    squares = jnp.sum(relaid_block * relaid_block, axis=1)
    square_total = lax.psum_scatter(squares, "col", scatter_dimension=0, tiled=True)
    row_norms = jnp.sqrt(square_total / full_width + epsilon)
    return (relaid_block, projected_share.T, row_norms)


def solution(mesh):
    placed = (P(("row", "col"), None), P(), P("col", "row"))
    return jax.shard_map(
        on_device,
        mesh=mesh,
        in_specs=placed,
        out_specs=(P("row", "col"), P(None, ("row", "col")), P(("row", "col"))),
        check_vma=False,
    )
```

profile of v0, /device:TPU:0, one launch (start us, length us, event | category | flops | bytes accessed | tf_op | source)
XLA Modules:
  0.0 133.8 jit_solution(3552242644922017772)
XLA Ops:
  7.2 0.0 copy-start
  7.2 1.0 dynamic-slice_reduce_fusion
  8.2 0.7 sort.51
  9.0 0.0 copy-done
  9.0 2.0 %gather_fusion = f32[4,8,16384]{2,1,0:T(8,128)} fusion(f32[4,8,16384]{2,1,0:T(8,128)S(1)} %bitcast.13, s32[1024]{0:T(1024)S(1)} %pad_clamp_fusion.1), kind=kCustom, calls=%fused_computation | custom fusion | bytes 4194320 | tf_op jit(solution)/shard_map/jit(_take)/gather | solution.py:21
  11.0 3.3 %broadcast_select_fusion = f32[4,8,8,2048]{3,1,2,0:T(8,128)} fusion(f32[4,8,8,2048]{3,1,2,0:T(8,128)} %bitcast.15, pred[4]{0:T(512)(128)(4,1)S(1)} %compare_and_fusion), kind=kLoop, calls=%fused_computation.4 | loop fusion | flops 524288 | bytes 4194308 | tf_op jit(solution)/shard_map/jit(_take)/select_n | solution.py:21
  14.3 0.0 copy-start.3
  14.3 0.0 copy-start.2
  14.3 0.0 copy-start.1
  14.3 7.5 %all-to-all-start = ((f32[32,8,2048]{2,1,0:T(8,128)}), f32[32,8,2048]{2,1,0:T(8,128)}, u32[]{:S(2)}, u32[]{:S(2)}) async-start(f32[32,8,2048]{2,1,0:T(8,128)} %bitcast.14), calls=%async_computation | async-start | bytes 4194304 | tf_op jit(solution)/shard_map/all_to_all | solution.py:24
  21.7 0.0 reduce-scatter.2.cloned.1.call-start
  21.8 0.0 copy-done.3
  21.8 0.6 dynamic-slice
  23.0 0.0 copy-done.2
  23.1 0.6 sort.49
  23.7 1.6 %sort.50 = (s32[32]{0:T(128)}, s32[32]{0:T(128)S(1)}) sort(s32[32]{0:T(128)S(1)} %dynamic-slice_bitcast_fusion, s32[32]{0:T(128)S(1)} %iota.12), dimensions={0}, to_apply=%region_1.2 | sort | flops 160 | bytes 512 | tf_op jit(solution)/shard_map/jit(argsort)/sort | solution.py:27
  25.3 0.1 broadcast_in_dim.32
  25.4 0.1 broadcast_in_dim.33
  25.5 0.0 copy-done.1
  25.5 16.7 %all_gather.3 = f32[2048,32]{0,1:T(8,128)S(1)} all-gather(f32[2048,8]{0,1:T(8,128)S(1)} %copy-done.1), channel_id=1, replica_groups=mesh['row'=4,'col'=8] {'row'}, dimensions={1}, use_global_device_ids=true | all-gather | bytes 327680 | tf_op jit(solution)/shard_map/all_gather | solution.py:30
  42.2 29.5 %all-to-all-done = f32[32,8,2048]{2,1,0:T(8,128)} async-done(((f32[32,8,2048]{2,1,0:T(8,128)}), f32[32,8,2048]{2,1,0:T(8,128)}, u32[]{:S(2)}, u32[]{:S(2)}) %all-to-all-start) | async-done | bytes 2097184 | tf_op jit(solution)/shard_map/all_to_all | solution.py:24
  71.7 3.6 %gather_fusion.1 = f32[32,8,2048]{2,1,0:T(8,128)} fusion(f32[32,8,2048]{2,1,0:T(8,128)} %all-to-all-done, s32[1024]{0:T(1024)S(1)} %pad_clamp_fusion), kind=kCustom, calls=%fused_computation.1 | custom fusion | bytes 4194432 | tf_op jit(solution)/shard_map/jit(_take)/gather | solution.py:28
  75.3 1.9 %multiply_reduce_fusion = f32[32,8]{1,0:T(8,128)S(1)} fusion(f32[32,8,2048]{2,1,0:T(8,128)} %gather_fusion.1, pred[32]{0:T(512)(128)(4,1)S(1)} %compare_and_fusion.1), kind=kLoop, calls=%fused_computation.3 | loop fusion | flops 1572608 | bytes 2098208 | tf_op jit(solution)/shard_map/reduce_sum | solution.py:42
  77.2 0.1 reduce_sum.12
  77.3 3.1 %bitcast_select_fusion = f32[256,2048]{1,0:T(8,128)} fusion(f32[32,8,2048]{2,1,0:T(8,128)} %gather_fusion.1, pred[256]{0:T(512)(128)(4,1)S(1)} %broadcast_in_dim.33), kind=kLoop, calls=%fused_computation.2 | loop fusion | flops 524288 | bytes 4194560 | tf_op jit(solution)/shard_map/jit(_take)/select_n | solution.py:28
  80.5 13.6 %all-reduce = f32[256]{0:T(256)S(1)} all-reduce(f32[256]{0:T(256)S(1)} %reduce_sum.12), channel_id=3, replica_groups=mesh['row'=4,'col'=8] {'col'}, use_global_device_ids=true, to_apply=%region_5.6.clone | all-reduce | flops 256 | bytes 2048
  94.0 4.0 %fusion.2 = f32[256,32]{1,0:T(8,128)} fusion(f32[256,2048]{1,0:T(8,128)} %bitcast_select_fusion, f32[2048,32]{0,1:T(8,128)S(1)} %all_gather.3), kind=kOutput, calls=%fused_computation.16 | convolution fusion | flops 201326592 | bytes 2392064 | tf_op jit(solution)/shard_map/dot_general | solution.py:32
  98.0 0.0 reduce-scatter.2.cloned.1.call-update
  98.1 0.6 fusion.1
  98.7 26.9 %reduce-scatter.2.cloned.1.call-done = f32[32,32]{1,0:T(8,128)} async-done(((f32[256,32]{1,0:T(8,128)}), f32[32,32]{1,0:T(8,128)}) %reduce-scatter.2.cloned.1.call-update) | async-done | bytes 4112 | tf_op jit(solution)/shard_map/reduce_scatter | solution.py:31
  125.5 1.4 %copy.8 = f32[32,32]{1,0:T(8,128)} copy(f32[32,32]{0,1:T(8,128)} %bitcast.16) | data formatting | bytes 8192
  (10 shorter events, 0.0 us)
Async XLA Ops:
  7.2 1.8 %copy-start = (f32[32,16384]{1,0:T(8,128)S(1)}, f32[32,16384]{1,0:T(8,128)}, u32[]{:S(2)}) copy-start(f32[32,16384]{1,0:T(8,128)} %param.3) | copy-start | bytes 6291460
  14.3 7.5 %copy-start.3 = (u32[32]{0:T(128)S(1)}, u32[32]{0:T(128)}, u32[]{:S(2)}) copy-start(u32[32]{0:T(128)} %constant.57) | copy-start | bytes 388
  14.3 8.8 %copy-start.2 = (s32[32,4]{0,1:T(4,128)S(1)}, s32[32,4]{0,1:T(4,128)}, u32[]{:S(2)}) copy-start(s32[32,4]{0,1:T(4,128)} %param.4) | copy-start | bytes 1540
  14.3 11.2 %copy-start.1 = (f32[2048,8]{0,1:T(8,128)S(1)}, f32[2048,8]{0,1:T(8,128)}, u32[]{:S(2)}) copy-start(f32[2048,8]{0,1:T(8,128)} %param.5) | copy-start | bytes 196612
  14.3 57.5 %all-to-all-start = ((f32[32,8,2048]{2,1,0:T(8,128)}), f32[32,8,2048]{2,1,0:T(8,128)}, u32[]{:S(2)}, u32[]{:S(2)}) async-start(f32[32,8,2048]{2,1,0:T(8,128)} %bitcast.14), calls=%async_computation | async-start | bytes 4194304 | tf_op jit(solution)/shard_map/all_to_all | solution.py:24
  21.7 103.8 %reduce-scatter.2.cloned.1.call-start = ((), (), s32[]{:S(2)}) async-start(), calls=%async_computation.2 | async-start | bytes 147456 | tf_op jit(solution)/shard_map/reduce_scatter | solution.py:31
Sparse Core Ops, SparseCore 0:
  98.2 27.3 reduce-scatter.1
where the time goes:
time: 134 us
  waiting for transfers between devices  56.4 us (42%)
  blocking collectives  30.3 us (23%)
  between operations  14.8 us (11%)
  other arithmetic  11.9 us (9%)
  local copies, waits for them, and re-layouts  8.86 us (7%)
  starting transfers between devices  7.5 us (6%)
  matrix products  3.99 us (3%)
    all_to_all x1, waiting for transfers between devices, on_device(): lax.all_to_all(flat_pieces, ('row', 'col'), split_axis=0, concat_axis=0,...  29.5 us
    reduce_scatter x1, waiting for transfers between devices, on_device(): lax.psum_scatter(jnp.dot(relaid_block, factor_full, precision=lax.Precisi...  26.9 us
    all_gather x1, blocking collectives, on_device(): factor_full = lax.all_gather(q_factor, 'row', axis=1, tiled=True)  16.7 us
    unnamed x1, blocking collectives  13.6 us
    all_to_all x1, starting transfers between devices, on_device(): lax.all_to_all(flat_pieces, ('row', 'col'), split_axis=0, concat_axis=0,...  7.45 us
    dot_general x1, matrix products, on_device(): jnp.dot(relaid_block, factor_full, precision=lax.Precision.HIGHEST, prefe...  3.99 us
    gather x1, local copies, waits for them, and re-layouts, on_device(): arranged = jnp.take(received, placement, axis=0)  3.56 us
    select_n x2, other arithmetic, on_device(): jnp.take(old_residual.reshape(row_count, group_rows, full_width), sending...  3.28 us
  transfers between devices with their start and end apart: 2, of which 2 were waited for; matrix products, arithmetic and copies ran while one was open for 3% of the time, Pallas kernels for 0%

commit v1 on v0

--- a/solution.py
+++ b/solution.py
@@ -27,7 +27,7 @@
     placement = jnp.argsort(arriving_ids)
     arranged = jnp.take(received, placement, axis=0)
     relaid_block = arranged.reshape(devices_all * group_rows, block_width)
-    factor_full = lax.all_gather(q_factor, "row", axis=1, tiled=True)
+    factor_full = jnp.concatenate(lax.all_gather(q_factor, "row"), axis=1)
     projected_share = lax.psum_scatter(
         jnp.dot(
             relaid_block,

time: 134 us -> 117 us (0.87)
  waiting for transfers between devices: 56.4 us -> 40.5 us
  matrix products: 3.99 us -> 2.49 us
    reduce_scatter x1, waiting for transfers between devices: 26.9 us -> 11 us  [on_device(): lax.psum_scatter(jnp.dot(relaid_block, factor_full, precision=lax.Precisi...]
    dot_general x1, matrix products: 3.99 us -> 2.49 us  [on_device(): jnp.dot(relaid_block, factor_full, precision=lax.Precision.HIGHEST, prefe...]
  transfers between devices with their start and end apart: 2 -> 2, of which waited for: 2 -> 2; matrix products, arithmetic and copies ran while one was open for 3% -> 6% of each run, Pallas kernels for 0% -> 0%
where the time goes in v1:
time: 117 us
  waiting for transfers between devices  40.5 us (35%)
  blocking collectives  30.4 us (26%)
  between operations  14.8 us (13%)
  other arithmetic  12.1 us (10%)
  local copies, waits for them, and re-layouts  9.04 us (8%)
  starting transfers between devices  7.5 us (6%)
  matrix products  2.49 us (2%)
    all_to_all x1, waiting for transfers between devices, on_device(): lax.all_to_all(flat_pieces, ('row', 'col'), split_axis=0, concat_axis=0,...  29.5 us
    all_gather x1, blocking collectives, on_device(): factor_full = jnp.concatenate(lax.all_gather(q_factor, 'row'), axis=1)  16.7 us
    unnamed x1, blocking collectives  13.6 us
    reduce_scatter x1, waiting for transfers between devices, on_device(): lax.psum_scatter(jnp.dot(relaid_block, factor_full, precision=lax.Precisi...  11 us
    all_to_all x1, starting transfers between devices, on_device(): lax.all_to_all(flat_pieces, ('row', 'col'), split_axis=0, concat_axis=0,...  7.45 us
    gather x1, local copies, waits for them, and re-layouts, on_device(): arranged = jnp.take(received, placement, axis=0)  3.62 us
    select_n x2, other arithmetic, on_device(): jnp.take(old_residual.reshape(row_count, group_rows, full_width), sending...  3.28 us
    select_n x2, other arithmetic, on_device(): arranged = jnp.take(received, placement, axis=0)  3.12 us
  transfers between devices with their start and end apart: 2, of which 2 were waited for; matrix products, arithmetic and copies ran while one was open for 6% of the time, Pallas kernels for 0%

profile of v1, /device:TPU:0, one launch (start us, length us, event | category | flops | bytes accessed | tf_op | source)
XLA Modules:
  0.0 116.7 jit_solution(15376447841465269885)
XLA Ops:
  7.2 0.0 copy-start
  7.2 1.0 dynamic-slice_reduce_fusion
  8.2 0.7 sort.51
  9.0 0.0 copy-done
  9.0 2.0 %gather_fusion = f32[4,8,16384]{2,1,0:T(8,128)} fusion(f32[4,8,16384]{2,1,0:T(8,128)S(1)} %bitcast.20, s32[1024]{0:T(1024)S(1)} %pad_clamp_fusion.1), kind=kCustom, calls=%fused_computation | custom fusion | bytes 4194320 | tf_op jit(solution)/shard_map/jit(_take)/gather | solution.py:21
  11.0 3.3 %broadcast_select_fusion = f32[4,8,8,2048]{3,1,2,0:T(8,128)} fusion(f32[4,8,8,2048]{3,1,2,0:T(8,128)} %bitcast.22, pred[4]{0:T(512)(128)(4,1)S(1)} %compare_and_fusion), kind=kLoop, calls=%fused_computation.8 | loop fusion | flops 524288 | bytes 4194308 | tf_op jit(solution)/shard_map/jit(_take)/select_n | solution.py:21
  14.3 0.0 copy-start.4
  14.3 0.0 copy-start.3
  14.3 0.0 copy-start.2
  14.3 7.5 %all-to-all-start = ((f32[32,8,2048]{2,1,0:T(8,128)}), f32[32,8,2048]{2,1,0:T(8,128)}, u32[]{:S(2)}, u32[]{:S(2)}) async-start(f32[32,8,2048]{2,1,0:T(8,128)} %bitcast.21), calls=%async_computation | async-start | bytes 4194304 | tf_op jit(solution)/shard_map/all_to_all | solution.py:24
  21.7 0.0 reduce-scatter.2.cloned.1.call-start
  21.8 0.0 copy-done.4
  21.8 0.6 dynamic-slice
  23.0 0.0 copy-done.3
  23.1 0.6 sort.49
  23.7 1.6 %sort.50 = (s32[32]{0:T(128)}, s32[32]{0:T(128)S(1)}) sort(s32[32]{0:T(128)S(1)} %dynamic-slice_bitcast_fusion, s32[32]{0:T(128)S(1)} %iota.12), dimensions={0}, to_apply=%region_1.2 | sort | flops 160 | bytes 512 | tf_op jit(solution)/shard_map/jit(argsort)/sort | solution.py:27
  25.3 0.1 broadcast_in_dim.32
  25.4 0.1 broadcast_in_dim.33
  25.5 0.0 copy-done.2
  25.5 16.7 %all-gather = f32[8192,8]{0,1:T(8,128)S(1)} all-gather(f32[2048,8]{0,1:T(8,128)S(1)} %copy-done.2), channel_id=2, replica_groups=mesh['row'=4,'col'=8] {'row'}, dimensions={0}, use_global_device_ids=true | all-gather | bytes 327680 | tf_op jit(solution)/shard_map/all_gather | solution.py:30
  42.2 29.5 %all-to-all-done = f32[32,8,2048]{2,1,0:T(8,128)} async-done(((f32[32,8,2048]{2,1,0:T(8,128)}), f32[32,8,2048]{2,1,0:T(8,128)}, u32[]{:S(2)}, u32[]{:S(2)}) %all-to-all-start) | async-done | bytes 2097184 | tf_op jit(solution)/shard_map/all_to_all | solution.py:24
  71.7 3.6 %gather_fusion.1 = f32[32,8,2048]{2,1,0:T(8,128)} fusion(f32[32,8,2048]{2,1,0:T(8,128)} %all-to-all-done, s32[1024]{0:T(1024)S(1)} %pad_clamp_fusion), kind=kCustom, calls=%fused_computation.1 | custom fusion | bytes 4194432 | tf_op jit(solution)/shard_map/jit(_take)/gather | solution.py:28
  75.4 0.0 copy-start.1
  75.4 2.1 %multiply_reduce_fusion = f32[32,8]{1,0:T(8,128)S(1)} fusion(f32[32,8,2048]{2,1,0:T(8,128)} %gather_fusion.1, pred[32]{0:T(512)(128)(4,1)S(1)} %compare_and_fusion.1), kind=kLoop, calls=%fused_computation.5 | loop fusion | flops 1572608 | bytes 2098208 | tf_op jit(solution)/shard_map/reduce_sum | solution.py:42
  77.5 0.1 copy-done.1
  77.6 2.5 %fusion = f32[256,32]{1,0:T(8,128)} fusion(f32[2048,32]{0,1:T(8,128)S(1)} %bitcast.23, f32[32,8,2048]{2,1,0:T(8,128)S(1)} %copy-done.1, pred[32]{0:T(512)(128)(4,1)S(1)} %compare_and_fusion.1), kind=kOutput, calls=%fused_computation.2 | convolution fusion | flops 201850880 | bytes 2392096 | tf_op jit(solution)/shard_map/dot_general | solution.py:32
  80.1 0.0 reduce-scatter.2.cloned.1.call-update
  80.1 0.1 reduce_sum.12
  80.2 3.1 %bitcast_select_fusion = f32[256,2048]{1,0:T(8,128)} fusion(f32[32,8,2048]{2,1,0:T(8,128)} %gather_fusion.1, pred[256]{0:T(512)(128)(4,1)S(1)} %broadcast_in_dim.33), kind=kLoop, calls=%fused_computation.4 | loop fusion | flops 524288 | bytes 4194560 | tf_op jit(solution)/shard_map/jit(_take)/select_n | solution.py:28
  83.3 13.6 %all-reduce = f32[256]{0:T(256)S(1)} all-reduce(f32[256]{0:T(256)S(1)} %reduce_sum.12), channel_id=4, replica_groups=mesh['row'=4,'col'=8] {'col'}, use_global_device_ids=true, to_apply=%region_5.6.clone | all-reduce | flops 256 | bytes 2048
  96.9 0.6 fusion.6
  97.5 11.0 %reduce-scatter.2.cloned.1.call-done = f32[32,32]{1,0:T(8,128)} async-done(((f32[256,32]{1,0:T(8,128)}), f32[32,32]{1,0:T(8,128)}) %reduce-scatter.2.cloned.1.call-update) | async-done | bytes 4112 | tf_op jit(solution)/shard_map/reduce_scatter | solution.py:31
  108.5 1.4 %copy.8 = f32[32,32]{1,0:T(8,128)} copy(f32[32,32]{0,1:T(8,128)} %bitcast.24) | data formatting | bytes 8192
  (10 shorter events, 0.0 us)
Async XLA Ops:
  7.2 1.8 %copy-start = (f32[32,16384]{1,0:T(8,128)S(1)}, f32[32,16384]{1,0:T(8,128)}, u32[]{:S(2)}) copy-start(f32[32,16384]{1,0:T(8,128)} %param.3) | copy-start | bytes 6291460
  14.3 7.5 %copy-start.4 = (u32[32]{0:T(128)S(1)}, u32[32]{0:T(128)}, u32[]{:S(2)}) copy-start(u32[32]{0:T(128)} %constant.57) | copy-start | bytes 388
  14.3 8.8 %copy-start.3 = (s32[32,4]{0,1:T(4,128)S(1)}, s32[32,4]{0,1:T(4,128)}, u32[]{:S(2)}) copy-start(s32[32,4]{0,1:T(4,128)} %param.4) | copy-start | bytes 1540
  14.3 11.2 %copy-start.2 = (f32[2048,8]{0,1:T(8,128)S(1)}, f32[2048,8]{0,1:T(8,128)}, u32[]{:S(2)}) copy-start(f32[2048,8]{0,1:T(8,128)} %param.5) | copy-start | bytes 196612
  14.3 57.5 %all-to-all-start = ((f32[32,8,2048]{2,1,0:T(8,128)}), f32[32,8,2048]{2,1,0:T(8,128)}, u32[]{:S(2)}, u32[]{:S(2)}) async-start(f32[32,8,2048]{2,1,0:T(8,128)} %bitcast.21), calls=%async_computation | async-start | bytes 4194304 | tf_op jit(solution)/shard_map/all_to_all | solution.py:24
  21.7 86.8 %reduce-scatter.2.cloned.1.call-start = ((), (), s32[]{:S(2)}) async-start(), calls=%async_computation.2 | async-start | bytes 147456 | tf_op jit(solution)/shard_map/reduce_scatter | solution.py:31
  75.4 2.2 %copy-start.1 = (f32[32,8,2048]{2,1,0:T(8,128)S(1)}, f32[32,8,2048]{2,1,0:T(8,128)}, u32[]{:S(2)}) copy-start(f32[32,8,2048]{2,1,0:T(8,128)} %gather_fusion.1) | copy-start | bytes 6291460
Sparse Core Ops, SparseCore 0:
  80.2 28.2 reduce-scatter.1
